TPU v7x, 32 devices: a whole 2x2x4 slice. The times are simulated.
32 devices in a mesh: front: 8 (over y, x, core), sub: 4 (over z).
Axes of the slice: x: 2, y: 2, z: 4, core: 2. Of those that a mesh axis runs over, the one named last changes fastest.
Arguments:
- row_values: float32 [4096, 1024], P(('front', 'sub')), may hold values from -0.12 to 0.12
- front_of_row: int32 [4096, 1], P(('front', 'sub')), may hold values from 0 to 7; in each aligned block of 128 rows (0 to 127, 128 to 255, ...) at most 32 rows name the same one
- child_factors: float32 [16, 512, 512], P('front', 'sub'), as said below
- child_columns: int32 [16, 512], P('front'), may hold values from 0 to 1023, as said below
- damping: float32 [8, 1024], P('front'), may hold values from 0.5 to 2
Outputs:
- front_factor: float32 [8, 1024, 1024], P('front', 'sub')
Inputs may be any that keep to these rules, and one draw needn't show every extreme that they name: `front_of_row`: among the 128 rows of one device, at most 32 name the same front, and some device's block reaches this bound. `child_factors`: each block is upper triangular with a positive diagonal. `child_columns`: each row names 512 distinct columns.
All inputs are finite; a program needn't handle non-finite values.
Results may differ from a plain program's by a relative error of at most 0.0003.
Values sent between devices are 32-bit elements; how exact they have to be, the bound alone decides.
A program may use at most 64 MiB of HBM per device.

v0:
```python
import jax
import jax.numpy as jnp
from jax import lax
from jax.sharding import PartitionSpec as P

HIGHEST = lax.Precision.HIGHEST


def cross_product(left_cols, right_cols):
    return lax.dot_general(
        left_cols,
        right_cols,
        (((0,), (0,)), ((), ())),
        precision=HIGHEST,
        preferred_element_type=jnp.float32,
    )


def local(row_values, front_of_row, child_factors, child_columns, damping):
    fronts = lax.axis_size("front")
    rows_held, front_width = row_values.shape
    capacity = 2 * rows_held // fronts
    destination = front_of_row[:, 0]
    onehot = (destination[:, None] == jnp.arange(fronts, dtype=jnp.int32)[None, :]).astype(
        jnp.int32
    )
    position = jnp.sum((jnp.cumsum(onehot, axis=0) - onehot) * onehot, axis=1)
    slot_of = destination * capacity + position
    source = (
        jnp.full((fronts * capacity,), rows_held, jnp.int32)
        .at[slot_of]
        .set(jnp.arange(rows_held, dtype=jnp.int32))
    )
    padded = jnp.concatenate([row_values, jnp.zeros((1, front_width), row_values.dtype)], axis=0)
    outgoing = padded[source]
    received = lax.all_to_all(outgoing, "front", split_axis=0, concat_axis=0, tiled=True)
    columns = jnp.arange(front_width, dtype=jnp.int32)
    spread = (child_columns[:, :, None] == columns[None, None, :]).astype(jnp.float32)
    placed = jnp.einsum(
        "jrc,jcf->jrf", child_factors, spread, precision=HIGHEST, preferred_element_type=jnp.float32
    )
    stacked = jnp.concatenate([placed.reshape(-1, front_width), received], axis=0)
    sub_count = lax.axis_size("sub")
    block_rows = front_width // sub_count
    own_index = lax.axis_index("sub")
    weight = damping[0]
    summed_gram = lax.psum(cross_product(stacked, stacked), "sub")
    summed_gram = summed_gram + jnp.diag(weight * weight)
    full_factor = jnp.linalg.cholesky(summed_gram).T
    own_rows = lax.dynamic_slice_in_dim(full_factor, own_index * block_rows, block_rows, 0)
    return own_rows[None]


def solution(mesh):
    in_specs = (
        P(("front", "sub"), None),
        P(("front", "sub"), None),
        P("front", "sub", None),
        P("front", None),
        P("front", None),
    )
    out_specs = P("front", "sub", None)
    return jax.shard_map(local, mesh=mesh, in_specs=in_specs, out_specs=out_specs, check_vma=False)
```

profile of v0, /device:TPU:0, one launch (start us, length us, event | category | flops | bytes accessed | tf_op | source)
XLA Modules:
  0.0 432.0 jit_solution(13834568773688344293)
XLA Ops:
  13.1 5.2 %all-to-all-start = ((f32[8,32,1024]{2,1,0:T(8,128)}), f32[8,32,1024]{2,1,0:T(8,128)S(1)}, u32[]{:S(2)}, u32[]{:S(2)}) async-start(f32[8,32,1024]{2,1,0:T(8,128)} %bitcast.5), calls=%async_computation | async-start | bytes 2097152 | tf_op jit(solution)/shard_map/all_to_all | solution.py:36
  20.0 13.7 %all-to-all-done = f32[8,32,1024]{2,1,0:T(8,128)S(1)} async-done(((f32[8,32,1024]{2,1,0:T(8,128)}), f32[8,32,1024]{2,1,0:T(8,128)S(1)}, u32[]{:S(2)}, u32[]{:S(2)}) %all-to-all-start) | async-done | bytes 1048608 | tf_op jit(solution)/shard_map/all_to_all | solution.py:36
  33.7 8.4 %fusion.2 = f32[1024,1024]{0,1:T(8,128)} fusion(f32[256,1024]{1,0:T(8,128)S(1)} %bitcast.58, f32[256,1024]{1,0:T(8,128)S(1)} %bitcast.63), kind=kOutput, calls=%fused_computation.8 | convolution fusion | flops 6442975232 | bytes 6291456 | tf_op jit(solution)/shard_map/dot_general | solution.py:10
  42.9 153.9 %all-reduce.4.cloned.1.call-done = f32[1024,1024]{0,1:T(8,128)} async-done(((f32[1024,1024]{0,1:T(8,128)}), f32[1024,1024]{0,1:T(8,128)}) %all-reduce.4.cloned.1.call-update) | async-done | bytes 4194320 | tf_op jit(solution)/shard_map/psum | solution.py:47
  196.7 4.8 %select_add_fusion = f32[1024,1024]{0,1:T(8,128)} fusion(f32[1024,1024]{0,1:T(8,128)} %all-reduce.4.cloned.1.call-done, f32[1024]{0:T(1024)S(1)} %bitcast.59), kind=kLoop, calls=%fused_computation.4 | loop fusion | flops 3145728 | bytes 8392704 | tf_op jit(solution)/shard_map/add | solution.py:48
  201.6 5.5 %copy.7 = f32[1024,1024]{1,0:T(8,128)} copy(f32[1024,1024]{0,1:T(8,128)} %select_add_fusion) | data formatting | bytes 8388608 | tf_op jit(solution)/shard_map/add | solution.py:48
  207.1 4.4 %fusion = f32[1024,1024]{1,0:T(8,128)S(1)} fusion(f32[1024,1024]{1,0:T(8,128)} %copy.7, f32[1024,1024]{0,1:T(8,128)} %all-reduce.4.cloned.1.call-done, f32[1024]{0:T(1024)S(1)} %bitcast.60), kind=kLoop, calls=%fused_computation.3 | loop fusion | flops 5242880 | bytes 12587008 | tf_op jit(solution)/shard_map/jit(cholesky)/div | solution.py:49
  213.5 11.7 %cholesky.224 = f32[128,128]{1,0:T(8,128)S(1)} custom-call(f32[128,128]{1,0:T(8,128)S(1)} %cholesky.580), custom_call_target="Cholesky" | custom-call | tf_op jit(solution)/shard_map/jit(cholesky)/cholesky | solution.py:49
  225.4 9.8 %custom-call.59 = f32[1,128,128]{1,2,0:T(8,128)S(1)} custom-call(f32[1,128,128]{2,1,0:T(8,128)S(1)} %get-tuple-element.18), custom_call_target="InvertDiagBlocksLowerTriangular" | custom-call | tf_op jit(solution)/shard_map/jit(cholesky)/cholesky | solution.py:49
  238.5 11.7 %cholesky.245 = f32[128,128]{1,0:T(8,128)S(1)} custom-call(f32[128,128]{1,0:T(8,128)S(1)} %cholesky.584), custom_call_target="Cholesky" | custom-call | tf_op jit(solution)/shard_map/jit(cholesky)/cholesky | solution.py:49
  253.2 9.8 %custom-call.60 = f32[1,128,128]{1,2,0:T(8,128)S(1)} custom-call(f32[1,128,128]{2,1,0:T(8,128)S(1)} %get-tuple-element.16), custom_call_target="InvertDiagBlocksLowerTriangular" | custom-call | tf_op jit(solution)/shard_map/jit(cholesky)/cholesky | solution.py:49
  268.5 11.7 %cholesky.469 = f32[128,128]{1,0:T(8,128)S(1)} custom-call(f32[128,128]{1,0:T(8,128)S(1)} %cholesky.589), custom_call_target="Cholesky" | custom-call | tf_op jit(solution)/shard_map/jit(cholesky)/cholesky | solution.py:49
  281.0 9.8 %custom-call.61 = f32[1,128,128]{1,2,0:T(8,128)S(1)} custom-call(f32[1,128,128]{2,1,0:T(8,128)S(1)} %get-tuple-element.14), custom_call_target="InvertDiagBlocksLowerTriangular" | custom-call | tf_op jit(solution)/shard_map/jit(cholesky)/cholesky | solution.py:49
  292.1 3.3 convolution_subtract_fusion.2
  295.4 11.7 %cholesky.488 = f32[128,128]{1,0:T(8,128)S(1)} custom-call(f32[128,128]{1,0:T(8,128)S(1)} %cholesky.594), custom_call_target="Cholesky" | custom-call | tf_op jit(solution)/shard_map/jit(cholesky)/cholesky | solution.py:49
  307.9 9.8 %custom-call.62 = f32[1,128,128]{1,2,0:T(8,128)S(1)} custom-call(f32[1,128,128]{2,1,0:T(8,128)S(1)} %get-tuple-element.12), custom_call_target="InvertDiagBlocksLowerTriangular" | custom-call | tf_op jit(solution)/shard_map/jit(cholesky)/cholesky | solution.py:49
  318.8 3.1 convolution_subtract_fusion.3
  322.0 11.9 %cholesky.507 = f32[128,128]{1,0:T(8,128)S(1)} custom-call(f32[128,128]{1,0:T(8,128)S(1)} %cholesky.599), custom_call_target="Cholesky" | custom-call | tf_op jit(solution)/shard_map/jit(cholesky)/cholesky | solution.py:49
  334.7 9.8 %custom-call.63 = f32[1,128,128]{1,2,0:T(8,128)S(1)} custom-call(f32[1,128,128]{2,1,0:T(8,128)S(1)} %get-tuple-element.10), custom_call_target="InvertDiagBlocksLowerTriangular" | custom-call | tf_op jit(solution)/shard_map/jit(cholesky)/cholesky | solution.py:49
  348.7 11.7 %cholesky.527 = f32[128,128]{1,0:T(8,128)S(1)} custom-call(f32[128,128]{1,0:T(8,128)S(1)} %cholesky.604), custom_call_target="Cholesky" | custom-call | tf_op jit(solution)/shard_map/jit(cholesky)/cholesky | solution.py:49
  361.2 9.8 %custom-call.64 = f32[1,128,128]{1,2,0:T(8,128)S(1)} custom-call(f32[1,128,128]{2,1,0:T(8,128)S(1)} %get-tuple-element.8), custom_call_target="InvertDiagBlocksLowerTriangular" | custom-call | tf_op jit(solution)/shard_map/jit(cholesky)/cholesky | solution.py:49
  374.9 11.7 %cholesky.547 = f32[128,128]{1,0:T(8,128)S(1)} custom-call(f32[128,128]{1,0:T(8,128)S(1)} %cholesky.609), custom_call_target="Cholesky" | custom-call | tf_op jit(solution)/shard_map/jit(cholesky)/cholesky | solution.py:49
  387.4 9.8 %custom-call.65 = f32[1,128,128]{1,2,0:T(8,128)S(1)} custom-call(f32[1,128,128]{2,1,0:T(8,128)S(1)} %get-tuple-element.6), custom_call_target="InvertDiagBlocksLowerTriangular" | custom-call | tf_op jit(solution)/shard_map/jit(cholesky)/cholesky | solution.py:49
  400.2 11.7 %cholesky.565 = f32[128,128]{1,0:T(8,128)S(1)} custom-call(f32[128,128]{1,0:T(8,128)S(1)} %convolution_subtract_fusion.6), custom_call_target="Cholesky" | custom-call | tf_op jit(solution)/shard_map/jit(cholesky)/cholesky | solution.py:49
  (75 shorter events, 47.5 us)
Async XLA Ops:
  6.5 11.9 %copy-start = (f32[2,128,512]{2,1,0:T(8,128)S(1)}, f32[2,128,512]{2,1,0:T(8,128)}, u32[]{:S(2)}) copy-start(f32[2,128,512]{2,1,0:T(8,128)} %param.7) | copy-start | bytes 1572868
  11.1 7.3 %copy-start.3 = (s32[2,512]{1,0:T(2,128)S(1)}, s32[2,512]{1,0:T(2,128)}, u32[]{:S(2)}) copy-start(s32[2,512]{1,0:T(2,128)} %param.8) | copy-start | bytes 12292
  13.1 20.6 %all-to-all-start = ((f32[8,32,1024]{2,1,0:T(8,128)}), f32[8,32,1024]{2,1,0:T(8,128)S(1)}, u32[]{:S(2)}, u32[]{:S(2)}) async-start(f32[8,32,1024]{2,1,0:T(8,128)} %bitcast.5), calls=%async_computation | async-start | bytes 2097152 | tf_op jit(solution)/shard_map/all_to_all | solution.py:36
  18.3 178.4 %all-reduce.4.cloned.1.call-start = ((), (), s32[]{:S(2)}) async-start(), calls=%async_computation.1 | async-start | bytes 8388608 | tf_op jit(solution)/shard_map/psum | solution.py:47
  42.2 0.7 copy-start.2
  211.6 1.9 copy-start.1
Sparse Core Ops, SparseCore 0:
  42.3 154.3 all-reduce.3
where the time goes:
time: 438 us; the launch traced here: 432 us
  other arithmetic  182 us (42%)
  waiting for transfers between devices  168 us (38%)
  matrix products  37.1 us (8%)
  local copies, waits for them, and re-layouts  21 us (5%)
  between operations  19.5 us (4%)
  starting transfers between devices  5.24 us (1%)
    another operation x30, other arithmetic, local(): full_factor = jnp.linalg.cholesky(summed_gram).T  167 us
    psum x1, waiting for transfers between devices, local(): summed_gram = lax.psum(cross_product(stacked, stacked), 'sub')  154 us
    another operation x14, matrix products, local(): full_factor = jnp.linalg.cholesky(summed_gram).T  27 us
    all_to_all x1, waiting for transfers between devices, local(): lax.all_to_all(outgoing, 'front', split_axis=0, concat_axis=0, tiled=True)  13.7 us
    another operation x25, local copies, waits for them, and re-layouts, local(): full_factor = jnp.linalg.cholesky(summed_gram).T  8.78 us
  transfers between devices with their start and end apart: 2, of which 2 were waited for; matrix products, arithmetic and copies ran while one was open for 0% of the time, Pallas kernels for 0%

commit v1 on v0

--- a/solution.py
+++ b/solution.py
@@ -44,7 +44,7 @@
     block_rows = front_width // sub_count
     own_index = lax.axis_index("sub")
     weight = damping[0]
-    summed_gram = lax.psum(cross_product(stacked, stacked), "sub")
+    summed_gram = jnp.sum(lax.all_gather(cross_product(stacked, stacked), "sub"), axis=0)
     summed_gram = summed_gram + jnp.diag(weight * weight)
     full_factor = jnp.linalg.cholesky(summed_gram).T
     own_rows = lax.dynamic_slice_in_dim(full_factor, own_index * block_rows, block_rows, 0)

time: 438 us -> 571 us (1.30)
  waiting for transfers between devices: 168 us -> 299 us
  other arithmetic: 182 us -> 191 us
    all_gather x0 -> x1, waiting for transfers between devices: none -> 286 us  [local(): lax.all_gather(cross_product(stacked, stacked), 'sub')]
    psum x1 -> x0, waiting for transfers between devices: 154 us -> none  [local(): summed_gram = lax.psum(cross_product(stacked, stacked), 'sub')]
    reduce_sum x0 -> x1, other arithmetic: none -> 10.3 us  [local(): jnp.sum(lax.all_gather(cross_product(stacked, stacked), 'sub'), axis=0)]
    another operation x25 -> x8, local copies, waits for them, and re-layouts: 8.78 us -> 2.55 us  [local(): full_factor = jnp.linalg.cholesky(summed_gram).T]
where the time goes in v1:
time: 571 us; the launch traced here: 564 us
  waiting for transfers between devices  299 us (52%)
  other arithmetic  191 us (33%)
  matrix products  33 us (6%)
  between operations  18.9 us (3%)
  local copies, waits for them, and re-layouts  16.1 us (3%)
    all_gather x1, waiting for transfers between devices, local(): lax.all_gather(cross_product(stacked, stacked), 'sub')  286 us
    another operation x30, other arithmetic, local(): full_factor = jnp.linalg.cholesky(summed_gram).T  172 us
    another operation x14, matrix products, local(): full_factor = jnp.linalg.cholesky(summed_gram).T  23.1 us
    all_to_all x1, waiting for transfers between devices, local(): lax.all_to_all(outgoing, 'front', split_axis=0, concat_axis=0, tiled=True)  13.7 us
  transfers between devices with their start and end apart: 2, of which 2 were waited for; matrix products, arithmetic and copies ran while one was open for 0% of the time, Pallas kernels for 0%

profile of v1, /device:TPU:0, one launch (start us, length us, event | category | flops | bytes accessed | tf_op | source)
XLA Modules:
  0.0 563.5 jit_solution(5917740742007001049)
XLA Ops:
  13.1 5.2 all-to-all-start
  20.0 13.7 %all-to-all-done = f32[8,32,1024]{2,1,0:T(8,128)S(1)} async-done(((f32[8,32,1024]{2,1,0:T(8,128)}), f32[8,32,1024]{2,1,0:T(8,128)S(1)}, u32[]{:S(2)}, u32[]{:S(2)}) %all-to-all-start) | async-done | bytes 1048608 | tf_op jit(solution)/shard_map/all_to_all | solution.py:36
  33.7 8.3 %fusion.1 = f32[1024,1024]{1,0:T(8,128)} fusion(f32[256,1024]{1,0:T(8,128)S(1)} %bitcast.60, f32[256,1024]{1,0:T(8,128)S(1)} %bitcast.64), kind=kOutput, calls=%fused_computation.7 | convolution fusion | flops 6442975232 | bytes 6291456 | tf_op jit(solution)/shard_map/dot_general | solution.py:10
  42.7 285.6 %all-gather.3.cloned.1.call-done = f32[4096,1024]{1,0:T(8,128)} async-done(((f32[1024,1024]{1,0:T(8,128)}), f32[4096,1024]{1,0:T(8,128)}) %all-gather.3.cloned.1.call-update) | async-done | bytes 16777232 | tf_op jit(solution)/shard_map/all_gather | solution.py:47
  328.4 10.3 %reduce_sum.24 = f32[1024,1024]{1,0:T(8,128)} reduce(f32[4,1024,1024]{2,1,0:T(8,128)} %bitcast.59, f32[]{:T(128)} %constant.277.clone.1), dimensions={0}, to_apply=%region_3.4 | reduce | flops 3145728 | bytes 20971524 | tf_op jit(solution)/shard_map/reduce_sum | solution.py:47
  338.7 5.5 copy.6
  344.2 4.5 add_multiply_fusion
  350.7 11.7 %cholesky.224 = f32[128,128]{1,0:T(8,128)S(1)} custom-call(f32[128,128]{1,0:T(8,128)S(1)} %cholesky.580), custom_call_target="Cholesky" | custom-call | tf_op jit(solution)/shard_map/jit(cholesky)/cholesky | solution.py:49
  362.4 2.5 cholesky.256
  364.9 9.8 %custom-call.59 = f32[1,128,128]{1,2,0:T(8,128)S(1)} custom-call(f32[1,128,128]{2,1,0:T(8,128)S(1)} %get-tuple-element.26), custom_call_target="InvertDiagBlocksLowerTriangular" | custom-call | tf_op jit(solution)/shard_map/jit(cholesky)/cholesky | solution.py:49
  374.8 2.4 constant_dynamic-update-slice_fusion.7
  378.7 12.1 %cholesky.245 = f32[128,128]{1,0:T(8,128)S(1)} custom-call(f32[128,128]{1,0:T(8,128)S(1)} %cholesky.584), custom_call_target="Cholesky" | custom-call | tf_op jit(solution)/shard_map/jit(cholesky)/cholesky | solution.py:49
  391.4 9.8 %custom-call.60 = f32[1,128,128]{1,2,0:T(8,128)S(1)} custom-call(f32[1,128,128]{2,1,0:T(8,128)S(1)} %get-tuple-element.23), custom_call_target="InvertDiagBlocksLowerTriangular" | custom-call | tf_op jit(solution)/shard_map/jit(cholesky)/cholesky | solution.py:49
  404.6 11.7 %cholesky.469 = f32[128,128]{1,0:T(8,128)S(1)} custom-call(f32[128,128]{1,0:T(8,128)S(1)} %cholesky.589), custom_call_target="Cholesky" | custom-call | tf_op jit(solution)/shard_map/jit(cholesky)/cholesky | solution.py:49
  417.5 9.8 %custom-call.61 = f32[1,128,128]{1,2,0:T(8,128)S(1)} custom-call(f32[1,128,128]{2,1,0:T(8,128)S(1)} %get-tuple-element.20), custom_call_target="InvertDiagBlocksLowerTriangular" | custom-call | tf_op jit(solution)/shard_map/jit(cholesky)/cholesky | solution.py:49
  430.9 11.9 %cholesky.488 = f32[128,128]{1,0:T(8,128)S(1)} custom-call(f32[128,128]{1,0:T(8,128)S(1)} %cholesky.594), custom_call_target="Cholesky" | custom-call | tf_op jit(solution)/shard_map/jit(cholesky)/cholesky | solution.py:49
  444.0 9.8 %custom-call.62 = f32[1,128,128]{1,2,0:T(8,128)S(1)} custom-call(f32[1,128,128]{2,1,0:T(8,128)S(1)} %get-tuple-element.17), custom_call_target="InvertDiagBlocksLowerTriangular" | custom-call | tf_op jit(solution)/shard_map/jit(cholesky)/cholesky | solution.py:49
  457.3 11.7 %cholesky.507 = f32[128,128]{1,0:T(8,128)S(1)} custom-call(f32[128,128]{1,0:T(8,128)S(1)} %cholesky.599), custom_call_target="Cholesky" | custom-call | tf_op jit(solution)/shard_map/jit(cholesky)/cholesky | solution.py:49
  470.3 10.0 %custom-call.63 = f32[1,128,128]{1,2,0:T(8,128)S(1)} custom-call(f32[1,128,128]{2,1,0:T(8,128)S(1)} %get-tuple-element.14), custom_call_target="InvertDiagBlocksLowerTriangular" | custom-call | tf_op jit(solution)/shard_map/jit(cholesky)/cholesky | solution.py:49
  483.6 11.7 %cholesky.527 = f32[128,128]{1,0:T(8,128)S(1)} custom-call(f32[128,128]{1,0:T(8,128)S(1)} %cholesky.604), custom_call_target="Cholesky" | custom-call | tf_op jit(solution)/shard_map/jit(cholesky)/cholesky | solution.py:49
  496.6 9.8 %custom-call.64 = f32[1,128,128]{1,2,0:T(8,128)S(1)} custom-call(f32[1,128,128]{2,1,0:T(8,128)S(1)} %get-tuple-element.11), custom_call_target="InvertDiagBlocksLowerTriangular" | custom-call | tf_op jit(solution)/shard_map/jit(cholesky)/cholesky | solution.py:49
  509.4 11.9 %cholesky.547 = f32[128,128]{1,0:T(8,128)S(1)} custom-call(f32[128,128]{1,0:T(8,128)S(1)} %cholesky.609), custom_call_target="Cholesky" | custom-call | tf_op jit(solution)/shard_map/jit(cholesky)/cholesky | solution.py:49
  522.6 9.8 %custom-call.65 = f32[1,128,128]{1,2,0:T(8,128)S(1)} custom-call(f32[1,128,128]{2,1,0:T(8,128)S(1)} %get-tuple-element.8), custom_call_target="InvertDiagBlocksLowerTriangular" | custom-call | tf_op jit(solution)/shard_map/jit(cholesky)/cholesky | solution.py:49
  535.0 11.7 %cholesky.565 = f32[128,128]{1,0:T(8,128)S(1)} custom-call(f32[128,128]{1,0:T(8,128)S(1)} %convolution_subtract_fusion.6), custom_call_target="Cholesky" | custom-call | tf_op jit(solution)/shard_map/jit(cholesky)/cholesky | solution.py:49
  (59 shorter events, 43.3 us)
Async XLA Ops:
  6.5 11.9 %copy-start = (f32[2,128,512]{2,1,0:T(8,128)S(1)}, f32[2,128,512]{2,1,0:T(8,128)}, u32[]{:S(2)}) copy-start(f32[2,128,512]{2,1,0:T(8,128)} %param.7) | copy-start | bytes 1572868
  11.1 7.3 %copy-start.3 = (s32[2,512]{1,0:T(2,128)S(1)}, s32[2,512]{1,0:T(2,128)}, u32[]{:S(2)}) copy-start(s32[2,512]{1,0:T(2,128)} %param.8) | copy-start | bytes 12292
  13.1 20.6 %all-to-all-start = ((f32[8,32,1024]{2,1,0:T(8,128)}), f32[8,32,1024]{2,1,0:T(8,128)S(1)}, u32[]{:S(2)}, u32[]{:S(2)}) async-start(f32[8,32,1024]{2,1,0:T(8,128)} %bitcast.5), calls=%async_computation | async-start | bytes 2097152 | tf_op jit(solution)/shard_map/all_to_all | solution.py:36
  18.3 310.0 %all-gather.3.cloned.1.call-start = ((), (), s32[]{:S(2)}) async-start(), calls=%async_computation.1 | async-start | bytes 20971520 | tf_op jit(solution)/shard_map/all_gather | solution.py:47
  42.0 0.7 copy-start.2
  348.8 1.9 copy-start.1
Sparse Core Ops, SparseCore 0:
  42.2 286.1 all-gather.2
